TPU v7x, 128 devices: a whole 4x4x4 slice. The times are simulated.
128 devices in a mesh: rows: 128 (over z, y, x, core).
Axes of the slice: x: 4, y: 4, z: 4, core: 2. Of those that a mesh axis runs over, the one named last changes fastest.
Arguments:
- events: float32 [4, 32, 1048576], P(None, None, 'rows'), may hold values from -8 to 8
- keep_indicator: int32 [4, 1048576], P(None, 'rows'), may hold values from 0 to 1, as said below
Outputs:
- lagging_mean: float32 [4, 32, 1048576], P(None, None, 'rows')
- deviation: float32 [4, 32, 1048576], P(None, None, 'rows')
Inputs may be any that keep to these rules, and one draw needn't show every extreme that they name: `keep_indicator`: in each table, each of the 128 aligned blocks of 8192 rows holds at least 4096 survivors, and some block holds exactly 4096.
All inputs are finite; a program needn't handle non-finite values.
Results may differ from a plain program's by a relative error of at most 0.0003.
Values sent between devices are 32-bit elements; how exact they have to be, the bound alone decides.
A program may use at most 128 MiB of HBM per device.

v0:
```python
import functools

import jax
import jax.numpy as jnp
from jax import lax
from jax.experimental import pallas as pl
from jax.experimental.pallas import tpu as pltpu
from jax.sharding import PartitionSpec as P

SPAN = 4096
LANES = 128
GROUP = 16
GRANT = 16 * 2**20
MESH = pl.DeviceIdType.MESH
F32, BF16, I32 = jnp.float32, jnp.bfloat16, jnp.int32


def iota(shape, axis):
    return lax.broadcasted_iota(I32, shape, axis)


def lane_gather(values, index):
    return jnp.take_along_axis(values, index, axis=1, mode="promise_in_bounds")


def index_kernel(tiles, keep_ref, rank_ref, slot_ref, scalars_ref, flags):
    streams = keep_ref.shape[0]
    rows = streams * tiles
    for s in range(streams):
        for t in range(tiles):
            flags[s * tiles + t : s * tiles + t + 1, :] = keep_ref[s : s + 1, t * LANES : (t + 1) * LANES]
    kept = flags[...].astype(F32).astype(BF16)
    square = (LANES, LANES)
    upper = (iota(square, 0) <= iota(square, 1)).astype(F32).astype(BF16)
    ones = jnp.ones(square, BF16)
    within = jnp.dot(kept, upper, preferred_element_type=F32)
    counts = jnp.dot(kept, ones, preferred_element_type=F32).astype(BF16)
    grid = (rows, rows)
    same = (iota(grid, 0) // tiles) == (iota(grid, 1) // tiles)
    below = (same & (iota(grid, 1) < iota(grid, 0))).astype(F32).astype(BF16)
    above = (same & (iota(grid, 0) < iota(grid, 1))).astype(F32).astype(BF16)
    start = jnp.dot(below, counts, preferred_element_type=F32).astype(I32)
    within = within.astype(I32)
    rank_ref[...] = start + within
    lane = iota((rows, LANES), 1)
    wanted = ((lane - start - 1) & (LANES - 1)) + 1
    position = jnp.zeros((rows, LANES), I32)
    step = LANES // 2
    while step:
        seen = lane_gather(within, position + (step - 1))
        position = jnp.where(seen < wanted, position + step, position)
        step //= 2
    slot_ref[...] = position
    contract = (((1,), (1,)), ((), ()))
    first = (iota((8, LANES), 1) == 0).astype(F32).astype(BF16)
    count_row = lax.dot_general(jnp.ones((8, LANES), BF16), kept, contract, preferred_element_type=F32)
    first_row = lax.dot_general(first, kept, contract, preferred_element_type=F32)
    count_row = count_row.astype(BF16)
    start_row = jnp.dot(count_row, above, preferred_element_type=F32)
    total_row = jnp.dot(count_row, same.astype(F32).astype(BF16), preferred_element_type=F32)
    which = iota((8, rows), 0)
    row = jnp.where(which == 0, start_row, jnp.where(which == 1, total_row, start_row + first_row))
    scalars_ref[...] = row.astype(I32)


def head_kernel(count, tiles, group, scalars_ref, events_ref, keep_ref, after_ref, prefix_ref, before_ref, *scratch):
    mine, slots, send_sems, recv_sems = scratch
    streams, cols, rows = events_ref.shape
    width = streams * cols
    me = lax.axis_index("rows")
    barrier = pltpu.get_barrier_semaphore()

    def greet(j, carry):
        @pl.when(j < me)
        def _():
            pl.semaphore_signal(barrier, inc=1, device_id=(j,), device_id_type=MESH)

        return carry

    lax.fori_loop(0, count, greet, 0)
    span = group * LANES

    def masked(s, g):
        columns = pl.ds(pl.multiple_of(g * span, span), span)
        return jnp.where(keep_ref[s : s + 1, columns] != 0, events_ref[s, :, columns], 0.0)

    totals = []
    for s in range(streams):

        def add(g, total, s=s):
            values = masked(s, g)
            parts = [values[:, i * LANES : (i + 1) * LANES] for i in range(group)]
            while len(parts) > 1:
                parts = [parts[i] + parts[i + 1] for i in range(0, len(parts), 2)]
            return total + parts[0]

        totals.append(lax.fori_loop(0, tiles // group, add, jnp.zeros((cols, LANES), F32), unroll=True))
    sums = lax.dot_general(
        jnp.ones((8, LANES), F32),
        jnp.concatenate(totals, axis=0),
        (((1,), (1,)), ((), ())),
        precision=lax.Precision.HIGHEST,
        preferred_element_type=F32,
    )
    row, column = iota((8, width), 0), iota((8, width), 1)
    counts = jnp.zeros((8, width), F32)
    for s in range(streams):
        counts = jnp.where(column // cols == s, scalars_ref[1, s * tiles].astype(F32), counts)
    mine[...] = jnp.where(row == 0, sums, counts)
    before_ref[...] = jnp.zeros((8, width), F32)

    @pl.when(me < count - 1)
    def _():
        pl.semaphore_wait(barrier, count - 1 - me)

    def copy(j, sender):
        return pltpu.make_async_remote_copy(
            src_ref=mine,
            dst_ref=slots.at[sender],
            send_sem=send_sems.at[j],
            recv_sem=recv_sems.at[sender],
            device_id=(j,),
            device_id_type=MESH,
        )

    def send(j, carry):
        @pl.when(j > me)
        def _():
            copy(j, me).start()

        return carry

    lax.fori_loop(0, count, send, 0)

    shape = (2 * LANES, 2 * LANES)
    weights = (((iota(shape, 0) & (LANES - 1)) <= iota(shape, 1)).astype(F32)).astype(BF16)
    for s in range(1, streams):

        def accumulate(g, total, s=s):
            values = masked(s, g)
            high = values.astype(BF16)
            low = (values - high.astype(F32)).astype(BF16)
            left = jnp.concatenate([high[:, i * LANES : (i + 1) * LANES] for i in range(group)], axis=0)
            right = jnp.concatenate([low[:, i * LANES : (i + 1) * LANES] for i in range(group)], axis=0)
            out = jnp.dot(jnp.concatenate([left, right], axis=1), weights, preferred_element_type=F32)
            for i in range(group):
                piece = out[i * cols : (i + 1) * cols]
                prefix_ref[(s - 1) * tiles + g * group + i] = piece[:, :LANES] + total
                total = total + piece[:, LANES:]
            return total

        lax.fori_loop(0, tiles // group, accumulate, jnp.zeros((cols, LANES), F32))

    def receive(j, carry):
        @pl.when(j < me)
        def _():
            copy(j, j).wait_recv()
            before_ref[...] += slots[j]

        return carry

    def finish(j, carry):
        @pl.when(j > me)
        def _():
            copy(j, me).wait_send()

        return carry

    lax.fori_loop(0, count, receive, 0)
    lax.fori_loop(0, count, finish, 0)


def pack_kernel(s, tiles, scalars_ref, prefix_ref, slot_ref, *rest):
    table_ref, send_ref = rest[-2:]
    cols = prefix_ref.shape[1]
    lane = iota((cols, LANES), 1)
    current = jnp.zeros((cols, LANES), F32)
    for t in range(tiles):
        order = jnp.broadcast_to(slot_ref[s * tiles + t : s * tiles + t + 1, :], (cols, LANES))
        packed = lane_gather(prefix_ref[(s - 1) * tiles + t], order)
        begin = scalars_ref[0, s * tiles + t] + 1
        block = begin // LANES
        merged = jnp.where(lane >= begin - block * LANES, packed, current)
        table_ref[block] = merged
        if t == tiles - 1:
            table_ref[block + 1] = packed
        else:
            following = (scalars_ref[0, s * tiles + t + 1] + 1) // LANES
            current = jnp.where(following > block, packed, merged)
    last = prefix_ref[s * tiles - 1]
    total = lane_gather(last, jnp.full((cols, LANES), LANES - 1, I32))
    base = scalars_ref[1, s * tiles] - SPAN
    origin = base // LANES
    offset = base - origin * LANES
    turn = (lane + offset) & (LANES - 1)
    below = table_ref[origin]
    for m in range(SPAN // LANES):
        above = table_ref[origin + m + 1]
        send_ref[m] = lane_gather(jnp.where(lane >= offset, below, above), turn) - total
        below = above


def first_pack_kernel(s, tiles, group, scalars_ref, events_ref, keep_ref, slot_ref, *rest):
    prefix_ref, table_ref, send_ref = rest[-3:]
    cols = prefix_ref.shape[1]
    lane = iota((cols, LANES), 1)
    shape = (2 * LANES, 2 * LANES)
    weights = (((iota(shape, 0) & (LANES - 1)) <= iota(shape, 1)).astype(F32)).astype(BF16)
    total = jnp.zeros((cols, LANES), F32)
    current = jnp.zeros((cols, LANES), F32)
    for g in range(tiles // group):
        left, right = [], []
        for i in range(group):
            columns = slice((g * group + i) * LANES, (g * group + i + 1) * LANES)
            values = jnp.where(keep_ref[s : s + 1, columns] != 0, events_ref[s, :, columns], 0.0)
            high = values.astype(BF16)
            left.append(high)
            right.append((values - high.astype(F32)).astype(BF16))
        pair = jnp.concatenate([jnp.concatenate(left, axis=0), jnp.concatenate(right, axis=0)], axis=1)
        sums = jnp.dot(pair, weights, preferred_element_type=F32)
        for i in range(group):
            t = g * group + i
            piece = sums[i * cols : (i + 1) * cols]
            running = piece[:, :LANES] + total
            total = total + piece[:, LANES:]
            prefix_ref[t] = running
            order = jnp.broadcast_to(slot_ref[s * tiles + t : s * tiles + t + 1, :], (cols, LANES))
            packed = lane_gather(running, order)
            begin = scalars_ref[0, s * tiles + t] + 1
            block = begin // LANES
            merged = jnp.where(lane >= begin - block * LANES, packed, current)
            table_ref[block] = merged
            if t == tiles - 1:
                table_ref[block + 1] = packed
            else:
                following = (scalars_ref[0, s * tiles + t + 1] + 1) // LANES
                current = jnp.where(following > block, packed, merged)
    base = scalars_ref[1, s * tiles] - SPAN
    origin = base // LANES
    offset = base - origin * LANES
    turn = (lane + offset) & (LANES - 1)
    below = table_ref[origin]
    for m in range(SPAN // LANES):
        above = table_ref[origin + m + 1]
        send_ref[m] = lane_gather(jnp.where(lane >= offset, below, above), turn) - total
        below = above


def spread_kernel(s, tiles, group, scalars_ref, before_ref, rank_ref, prefix_ref, table_ref, tail_ref, *rest):
    mean_ref, deviation_ref, means, deviations, inverse, sems = rest[-6:]
    cols = prefix_ref.shape[1]
    back = SPAN // LANES
    width = before_ref.shape[1]
    mine = iota((cols, width), 1) == iota((cols, width), 0) + s * cols
    column = jnp.sum(jnp.where(mine, before_ref[0:1, :], 0.0), axis=1, keepdims=True)
    before = jnp.broadcast_to(column, (cols, LANES))
    first = iota((1, width), 1) == s * cols
    earlier = jnp.sum(jnp.where(first, before_ref[1:2, :], 0.0), axis=1, keepdims=True)
    ranks = rank_ref[s * tiles : (s + 1) * tiles, :]
    inverse[...] = 1.0 / jnp.maximum(earlier + ranks.astype(F32), 1.0)
    lane = iota((cols, LANES), 1)

    def fetch(block):
        old = tail_ref[jnp.minimum(block, back - 1)]
        new = table_ref[jnp.maximum(block - back, 0)]
        return jnp.where(block < back, old, new)

    copies = []
    for g in range(tiles // group):
        for i in range(group):
            t = g * group + i
            begin = scalars_ref[2, s * tiles + t]
            block = begin // LANES
            mixed = jnp.where(lane >= begin - block * LANES, fetch(block), fetch(block + 1))
            order = jnp.broadcast_to(rank_ref[s * tiles + t : s * tiles + t + 1, :] & (LANES - 1), (cols, LANES))
            running = prefix_ref[max(s - 1, 0) * tiles + t]
            mean = (running - lane_gather(mixed, order)) * (1.0 / SPAN)
            columns = slice(t * LANES, (t + 1) * LANES)
            means[:, columns] = mean
            deviations[:, columns] = mean - (running + before) * inverse[t : t + 1, :]
        part = pl.ds(g * group * LANES, group * LANES)
        for k, (source, target) in enumerate(((means, mean_ref), (deviations, deviation_ref))):
            copy = pltpu.make_async_copy(source.at[:, part], target.at[s, :, part], sems.at[k, g])
            copy.start()
            copies.append(copy)
    for copy in copies:
        copy.wait()


def per_device(count, events, keep):
    streams, cols, rows = events.shape
    tiles = rows // LANES
    back = SPAN // LANES
    everything = streams * tiles
    width = streams * cols
    group = min(GROUP, tiles)
    smem = pl.BlockSpec(memory_space=pltpu.SMEM)
    vmem = pl.BlockSpec(memory_space=pltpu.VMEM)
    anywhere = pl.BlockSpec(memory_space=pl.ANY)
    cost = pl.CostEstimate(flops=10**9, bytes_accessed=8 * 2**20, transcendentals=0)
    params = pltpu.CompilerParams(vmem_limit_bytes=GRANT)

    rank, slot, scalars = pl.pallas_call(
        functools.partial(index_kernel, tiles),
        out_shape=(
            jax.ShapeDtypeStruct((everything, LANES), I32),
            jax.ShapeDtypeStruct((everything, LANES), I32),
            jax.ShapeDtypeStruct((8, everything), I32),
        ),
        scratch_shapes=[pltpu.VMEM((everything, LANES), I32)],
        cost_estimate=cost,
        compiler_params=params,
        name="index",
    )(keep)

    links = [(i, i + 1) for i in range(count - 1)]
    first, table, send = pl.pallas_call(
        functools.partial(first_pack_kernel, 0, tiles, group),
        in_specs=[smem, vmem, vmem, vmem],
        out_specs=[vmem] * 3,
        out_shape=[
            jax.ShapeDtypeStruct((tiles, cols, LANES), F32),
            jax.ShapeDtypeStruct((tiles + 2, cols, LANES), F32),
            jax.ShapeDtypeStruct((back, cols, LANES), F32),
        ],
        cost_estimate=cost,
        compiler_params=params,
        name="pack0",
    )(scalars, events, keep, slot)
    tables, tails = [table], [lax.ppermute(send, "rows", links)]

    prefix, before = pl.pallas_call(
        functools.partial(head_kernel, count, tiles, group),
        in_specs=[smem, vmem, vmem, anywhere],
        out_specs=[vmem, vmem],
        out_shape=[
            jax.ShapeDtypeStruct((everything - tiles, cols, LANES), F32),
            jax.ShapeDtypeStruct((8, width), F32),
        ],
        scratch_shapes=[
            pltpu.VMEM((8, width), F32),
            pltpu.VMEM((count, 8, width), F32),
            pltpu.SemaphoreType.DMA((count,)),
            pltpu.SemaphoreType.DMA((count,)),
        ],
        compiler_params=pltpu.CompilerParams(collective_id=0, has_side_effects=True, vmem_limit_bytes=GRANT),
        name="head",
    )(scalars, events, keep, table)

    for s in range(1, streams):
        table, send = pl.pallas_call(
            functools.partial(pack_kernel, s, tiles),
            in_specs=[smem, vmem, vmem] + [anywhere] * (s > 0),
            out_specs=[vmem, vmem],
            out_shape=[
                jax.ShapeDtypeStruct((tiles + 2, cols, LANES), F32),
                jax.ShapeDtypeStruct((back, cols, LANES), F32),
            ],
            cost_estimate=cost,
            compiler_params=params,
            name=f"pack{s}",
        )(scalars, prefix, slot, *tables[-1:])
        tails.append(lax.ppermute(send, "rows", [(i, i + 1) for i in range(count - 1)]))
        tables.append(table)

    outs = ()
    for s in range(streams):
        outs = pl.pallas_call(
            functools.partial(spread_kernel, s, tiles, group),
            in_specs=[smem] + [vmem] * 5 + [anywhere] * len(outs),
            out_specs=[anywhere] * 2,
            out_shape=[jax.ShapeDtypeStruct(events.shape, F32)] * 2,
            scratch_shapes=[
                pltpu.VMEM((cols, rows), F32),
                pltpu.VMEM((cols, rows), F32),
                pltpu.VMEM((tiles, LANES), F32),
                pltpu.SemaphoreType.DMA((2, tiles // group)),
            ],
            input_output_aliases={6: 0, 7: 1} if outs else {},
            cost_estimate=cost,
            compiler_params=params,
            name=f"spread{s}",
        )(scalars, before, rank, prefix if s else first, tables[s], tails[s], *outs)
    return tuple(outs)


def solution(mesh):
    return jax.shard_map(
        functools.partial(per_device, mesh.shape["rows"]),
        mesh=mesh,
        in_specs=(P(None, None, "rows"), P(None, "rows")),
        out_specs=(P(None, None, "rows"), P(None, None, "rows")),
        check_vma=False,
    )
```

profile of v0, /device:TPU:32, one launch (start us, length us, event | category | flops | bytes accessed | tf_op | source)
XLA Modules:
  0.0 61.5 jit_solution(10131244569935933343)
XLA Ops:
  0.6 0.0 copy-start.2
  0.6 0.9 %copy-done.2 = s32[4,8192]{1,0:T(4,128)S(1)} copy-done((s32[4,8192]{1,0:T(4,128)S(1)}, s32[4,8192]{1,0:T(4,128)}, u32[]{:S(2)}) %copy-start.2) | copy-done | bytes 131096
  1.5 1.0 %index.1 = (s32[256,128]{1,0:T(8,128)S(1)}, s32[256,128]{1,0:T(8,128)S(1)}, s32[8,256]{1,0:T(8,128)S(1)}) custom-call(s32[4,8192]{1,0:T(4,128)S(1)} %copy-done.2), custom_call_target="tpu_custom_call" | custom-call | flops 1000000000 | bytes 8388608 | tf_op jit(solution)/shard_map/index/pallas_call | solution.py:303
  2.5 0.0 copy-start
  2.5 2.2 %copy-done = f32[4,32,8192]{2,1,0:T(8,128)S(1)} copy-done((f32[4,32,8192]{2,1,0:T(8,128)S(1)}, f32[4,32,8192]{2,1,0:T(8,128)}, u32[]{:S(2)}) %copy-start) | copy-done | bytes 4194328
  4.7 0.0 copy-start.1
  4.7 1.7 %pack0.1 = (f32[64,32,128]{2,1,0:T(8,128)S(1)}, f32[66,32,128]{2,1,0:T(8,128)S(1)}, f32[32,32,128]{2,1,0:T(8,128)S(1)}) custom-call(s32[8,256]{1,0:T(8,128)S(1)} %get-tuple-element.22.scalars_ref, f32[4,32,8192]{2,1,0:T(8,128)S(1)} %copy-done, s32[4,8192]{1,0:T(4,128)S(1)} %copy-done.2, s32[256,128]{1,0:T(8,128)S(1)} %get-tuple-element.23.slot_ref), custom_call_target="tpu_custom_call" | custom-call | flops 1000000000 | bytes 8388608 | tf_op jit(solution)/shard_map/pack0/pallas_call | solution.py:317
  6.5 1.9 %collective-permute-start.3 = (f32[32,32,128]{2,1,0:T(8,128)S(1)}, f32[32,32,128]{2,1,0:T(8,128)S(1)}, u32[]{:S(2)}, u32[]{:S(2)}) collective-permute-start(f32[32,32,128]{2,1,0:T(8,128)S(1)} %get-tuple-element.35), channel_id=1, source_target_pairs={{0,1},{1,2},{2,3},{3,4},{4,5},{5,6},{6,7},{7,8},{8,9},{9,10},{10,1... | collective-permute-start | bytes 1572872 | tf_op jit(solution)/shard_map/ppermute | solution.py:330
  8.4 0.0 copy-done.1
  8.4 23.0 %head.1 = (f32[192,32,128]{2,1,0:T(8,128)S(1)}, f32[8,128]{1,0:T(8,128)S(1)}) custom-call(s32[8,256]{1,0:T(8,128)S(1)} %get-tuple-element.22.scalars_ref, f32[4,32,8192]{2,1,0:T(8,128)S(1)} %copy-done.1, s32[4,8192]{1,0:T(4,128)S(1)} %copy-done.2, f32[66,32,128]{2,1,0:T(8,128)S(1)} %get-tuple-element.24.after_ref.rest_0_.table_ref), custom_call_target="tpu_custom_call" | custom-call | tf_op jit(solution)/shard_map/head/pallas_call | solution.py:332
  31.4 1.4 %pack1.1 = (f32[66,32,128]{2,1,0:T(8,128)S(1)}, f32[32,32,128]{2,1,0:T(8,128)S(1)}) custom-call(s32[8,256]{1,0:T(8,128)S(1)} %get-tuple-element.22.scalars_ref, f32[192,32,128]{2,1,0:T(8,128)S(1)} %get-tuple-element.27.prefix_ref, s32[256,128]{1,0:T(8,128)S(1)} %get-tuple-element.23.slot_ref, f32[66,32,128]{2,1,0:T(8,128)S(1)} %get-tuple-element.24.after_ref.rest_0_.table_ref), custom_call_target="tpu_custom_call" | custom-call | flops 1000000000 | bytes 8388608 | tf_op jit(solution)/shard_map/pack1/pallas_call | solution.py:351
  32.9 2.0 %collective-permute-start.2 = (f32[32,32,128]{2,1,0:T(8,128)S(1)}, f32[32,32,128]{2,1,0:T(8,128)S(1)}, u32[]{:S(2)}, u32[]{:S(2)}) collective-permute-start(f32[32,32,128]{2,1,0:T(8,128)S(1)} %get-tuple-element.33), channel_id=1, source_target_pairs={{0,1},{1,2},{2,3},{3,4},{4,5},{5,6},{6,7},{7,8},{8,9},{9,10},{10,1... | collective-permute-start | bytes 1572872 | tf_op jit(solution)/shard_map/ppermute | solution.py:363
  34.9 1.4 %pack2.1 = (f32[66,32,128]{2,1,0:T(8,128)S(1)}, f32[32,32,128]{2,1,0:T(8,128)S(1)}) custom-call(s32[8,256]{1,0:T(8,128)S(1)} %get-tuple-element.22.scalars_ref, f32[192,32,128]{2,1,0:T(8,128)S(1)} %get-tuple-element.27.prefix_ref, s32[256,128]{1,0:T(8,128)S(1)} %get-tuple-element.23.slot_ref, f32[66,32,128]{2,1,0:T(8,128)S(1)} %get-tuple-element.28.rest_0_.table_ref), custom_call_target="tpu_custom_call" | custom-call | flops 1000000000 | bytes 8388608 | tf_op jit(solution)/shard_map/pack2/pallas_call | solution.py:351
  36.3 1.9 %collective-permute-start.1 = (f32[32,32,128]{2,1,0:T(8,128)S(1)}, f32[32,32,128]{2,1,0:T(8,128)S(1)}, u32[]{:S(2)}, u32[]{:S(2)}) collective-permute-start(f32[32,32,128]{2,1,0:T(8,128)S(1)} %get-tuple-element.32), channel_id=1, source_target_pairs={{0,1},{1,2},{2,3},{3,4},{4,5},{5,6},{6,7},{7,8},{8,9},{9,10},{10,1... | collective-permute-start | bytes 1572872 | tf_op jit(solution)/shard_map/ppermute | solution.py:363
  38.2 1.4 %pack3.1 = (f32[66,32,128]{2,1,0:T(8,128)S(1)}, f32[32,32,128]{2,1,0:T(8,128)S(1)}) custom-call(s32[8,256]{1,0:T(8,128)S(1)} %get-tuple-element.22.scalars_ref, f32[192,32,128]{2,1,0:T(8,128)S(1)} %get-tuple-element.27.prefix_ref, s32[256,128]{1,0:T(8,128)S(1)} %get-tuple-element.23.slot_ref, f32[66,32,128]{2,1,0:T(8,128)S(1)} %get-tuple-element.29.rest_0_.table_ref), custom_call_target="tpu_custom_call" | custom-call | flops 1000000000 | bytes 8388608 | tf_op jit(solution)/shard_map/pack3/pallas_call | solution.py:351
  39.7 1.9 %collective-permute-start = (f32[32,32,128]{2,1,0:T(8,128)S(1)}, f32[32,32,128]{2,1,0:T(8,128)S(1)}, u32[]{:S(2)}, u32[]{:S(2)}) collective-permute-start(f32[32,32,128]{2,1,0:T(8,128)S(1)} %get-tuple-element.31), channel_id=1, source_target_pairs={{0,1},{1,2},{2,3},{3,4},{4,5},{5,6},{6,7},{7,8},{8,9},{9,10},{10,1... | collective-permute-start | bytes 1572872 | tf_op jit(solution)/shard_map/ppermute | solution.py:363
  41.6 0.0 collective-permute-done.3.tail_ref
  41.6 2.7 %spread0.1 = (f32[4,32,8192]{2,1,0:T(8,128)}, f32[4,32,8192]{2,1,0:T(8,128)}) custom-call(s32[8,256]{1,0:T(8,128)S(1)} %get-tuple-element.22.scalars_ref, f32[8,128]{1,0:T(8,128)S(1)} %get-tuple-element.25.before_ref, s32[256,128]{1,0:T(8,128)S(1)} %get-tuple-element.26.rank_ref, f32[64,32,128]{2,1,0:T(8,128)S(1)} %get-tuple-element.34.prefix_ref, ...), custom_call_target="tpu_custom_call" | custom-call | flops 1000000000 | bytes 8388608 | tf_op jit(solution)/shard_map/spread0/pallas_call | solution.py:368
  44.3 3.2 %collective-permute-done.2.tail_ref = f32[32,32,128]{2,1,0:T(8,128)S(1)} collective-permute-done((f32[32,32,128]{2,1,0:T(8,128)S(1)}, f32[32,32,128]{2,1,0:T(8,128)S(1)}, u32[]{:S(2)}, u32[]{:S(2)}) %collective-permute-start.2) | collective-permute-done | bytes 524320 | tf_op jit(solution)/shard_map/ppermute | solution.py:363
  47.6 2.7 %spread1.1 = (f32[4,32,8192]{2,1,0:T(8,128)}, f32[4,32,8192]{2,1,0:T(8,128)}) custom-call(s32[8,256]{1,0:T(8,128)S(1)} %get-tuple-element.22.scalars_ref, f32[8,128]{1,0:T(8,128)S(1)} %get-tuple-element.25.before_ref, s32[256,128]{1,0:T(8,128)S(1)} %get-tuple-element.26.rank_ref, ...), custom_call_target="tpu_custom_call", output_to_operand_aliasing={{0}: (6, {}), {1}: (7, {})} | custom-call | flops 1000000000 | bytes 8388608 | tf_op jit(solution)/shard_map/spread1/pallas_call | solution.py:368
  50.3 2.9 %collective-permute-done.1.tail_ref = f32[32,32,128]{2,1,0:T(8,128)S(1)} collective-permute-done((f32[32,32,128]{2,1,0:T(8,128)S(1)}, f32[32,32,128]{2,1,0:T(8,128)S(1)}, u32[]{:S(2)}, u32[]{:S(2)}) %collective-permute-start.1) | collective-permute-done | bytes 524320 | tf_op jit(solution)/shard_map/ppermute | solution.py:363
  53.2 2.7 %spread2.1 = (f32[4,32,8192]{2,1,0:T(8,128)}, f32[4,32,8192]{2,1,0:T(8,128)}) custom-call(s32[8,256]{1,0:T(8,128)S(1)} %get-tuple-element.22.scalars_ref, f32[8,128]{1,0:T(8,128)S(1)} %get-tuple-element.25.before_ref, s32[256,128]{1,0:T(8,128)S(1)} %get-tuple-element.26.rank_ref, ...), custom_call_target="tpu_custom_call", output_to_operand_aliasing={{0}: (6, {}), {1}: (7, {})} | custom-call | flops 1000000000 | bytes 8388608 | tf_op jit(solution)/shard_map/spread2/pallas_call | solution.py:368
  55.9 2.9 %collective-permute-done.tail_ref = f32[32,32,128]{2,1,0:T(8,128)S(1)} collective-permute-done((f32[32,32,128]{2,1,0:T(8,128)S(1)}, f32[32,32,128]{2,1,0:T(8,128)S(1)}, u32[]{:S(2)}, u32[]{:S(2)}) %collective-permute-start) | collective-permute-done | bytes 524320 | tf_op jit(solution)/shard_map/ppermute | solution.py:363
  58.8 2.7 %spread3.1 = (f32[4,32,8192]{2,1,0:T(8,128)}, f32[4,32,8192]{2,1,0:T(8,128)}) custom-call(s32[8,256]{1,0:T(8,128)S(1)} %get-tuple-element.22.scalars_ref, f32[8,128]{1,0:T(8,128)S(1)} %get-tuple-element.25.before_ref, s32[256,128]{1,0:T(8,128)S(1)} %get-tuple-element.26.rank_ref, ...), custom_call_target="tpu_custom_call", output_to_operand_aliasing={{0}: (6, {}), {1}: (7, {})} | custom-call | flops 1000000000 | bytes 8388608 | tf_op jit(solution)/shard_map/spread3/pallas_call | solution.py:368
Async XLA Ops:
  0.6 0.9 %copy-start.2 = (s32[4,8192]{1,0:T(4,128)S(1)}, s32[4,8192]{1,0:T(4,128)}, u32[]{:S(2)}) copy-start(s32[4,8192]{1,0:T(4,128)} %keep_ref.5) | copy-start | bytes 393220
  2.5 2.2 %copy-start = (f32[4,32,8192]{2,1,0:T(8,128)S(1)}, f32[4,32,8192]{2,1,0:T(8,128)}, u32[]{:S(2)}) copy-start(f32[4,32,8192]{2,1,0:T(8,128)} %events_ref.3) | copy-start | bytes 12582916
  4.7 3.7 %copy-start.1 = (f32[4,32,8192]{2,1,0:T(8,128)S(1)}, f32[4,32,8192]{2,1,0:T(8,128)}, u32[]{:S(2)}) copy-start(f32[4,32,8192]{2,1,0:T(8,128)} %events_ref.3) | copy-start | bytes 12582916
  6.5 35.1 %collective-permute-start.3 = (f32[32,32,128]{2,1,0:T(8,128)S(1)}, f32[32,32,128]{2,1,0:T(8,128)S(1)}, u32[]{:S(2)}, u32[]{:S(2)}) collective-permute-start(f32[32,32,128]{2,1,0:T(8,128)S(1)} %get-tuple-element.35), channel_id=1, source_target_pairs={{0,1},{1,2},{2,3},{3,4},{4,5},{5,6},{6,7},{7,8},{8,9},{9,10},{10,1... | collective-permute-start | bytes 1572872 | tf_op jit(solution)/shard_map/ppermute | solution.py:330
  32.9 14.7 %collective-permute-start.2 = (f32[32,32,128]{2,1,0:T(8,128)S(1)}, f32[32,32,128]{2,1,0:T(8,128)S(1)}, u32[]{:S(2)}, u32[]{:S(2)}) collective-permute-start(f32[32,32,128]{2,1,0:T(8,128)S(1)} %get-tuple-element.33), channel_id=1, source_target_pairs={{0,1},{1,2},{2,3},{3,4},{4,5},{5,6},{6,7},{7,8},{8,9},{9,10},{10,1... | collective-permute-start | bytes 1572872 | tf_op jit(solution)/shard_map/ppermute | solution.py:363
  36.3 16.9 %collective-permute-start.1 = (f32[32,32,128]{2,1,0:T(8,128)S(1)}, f32[32,32,128]{2,1,0:T(8,128)S(1)}, u32[]{:S(2)}, u32[]{:S(2)}) collective-permute-start(f32[32,32,128]{2,1,0:T(8,128)S(1)} %get-tuple-element.32), channel_id=1, source_target_pairs={{0,1},{1,2},{2,3},{3,4},{4,5},{5,6},{6,7},{7,8},{8,9},{9,10},{10,1... | collective-permute-start | bytes 1572872 | tf_op jit(solution)/shard_map/ppermute | solution.py:363
  39.7 19.1 %collective-permute-start = (f32[32,32,128]{2,1,0:T(8,128)S(1)}, f32[32,32,128]{2,1,0:T(8,128)S(1)}, u32[]{:S(2)}, u32[]{:S(2)}) collective-permute-start(f32[32,32,128]{2,1,0:T(8,128)S(1)} %get-tuple-element.31), channel_id=1, source_target_pairs={{0,1},{1,2},{2,3},{3,4},{4,5},{5,6},{6,7},{7,8},{8,9},{9,10},{10,1... | collective-permute-start | bytes 1572872 | tf_op jit(solution)/shard_map/ppermute | solution.py:363
where the time goes:
time: 61.7 us; the launch traced here: 61.5 us
  Pallas kernels  40.8 us (66%)
  waiting for transfers between devices  9.1 us (15%)
  starting transfers between devices  7.79 us (13%)
  local copies, waits for them, and re-layouts  3.09 us (5%)
  between operations  0.76 us (1%)
    pallas_call x1, Pallas kernels, per_device(): pl.pallas_call(functools.partial(head_kernel, count, tiles, group), in_sp...  23 us
    pallas_call x4, Pallas kernels, per_device(): pl.pallas_call(functools.partial(spread_kernel, s, tiles, group), in_spec...  10.8 us
    ppermute x3, waiting for transfers between devices, per_device(): lax.ppermute(send, 'rows', [(i, i + 1) for i in range(count - 1)])  9.1 us
    ppermute x3, starting transfers between devices, per_device(): lax.ppermute(send, 'rows', [(i, i + 1) for i in range(count - 1)])  5.86 us
    pallas_call x3, Pallas kernels, per_device(): pl.pallas_call(functools.partial(pack_kernel, s, tiles), in_specs=[smem,...  4.26 us
    unnamed x6, local copies, waits for them, and re-layouts  3.09 us
    ppermute x1, starting transfers between devices, per_device(): tables, tails = ([table], [lax.ppermute(send, 'rows', links)])  1.92 us
    pallas_call x1, Pallas kernels, per_device(): pl.pallas_call(functools.partial(first_pack_kernel, 0, tiles, group), in_...  1.75 us
  transfers between devices with their start and end apart: 4, of which 3 were waited for; matrix products, arithmetic and copies ran while one was open for 0% of the time, Pallas kernels for 57%

commit v1 on v0

--- a/solution.py
+++ b/solution.py
@@ -63,9 +63,11 @@
     scalars_ref[...] = row.astype(I32)
 
 
-def head_kernel(count, tiles, group, scalars_ref, events_ref, keep_ref, after_ref, prefix_ref, before_ref, *scratch):
-    mine, slots, send_sems, recv_sems = scratch
-    streams, cols, rows = events_ref.shape
+def head_kernel(count, tiles, scalars_ref, *refs):
+    prefix_refs = refs[:-5]
+    before_ref, mine, slots, send_sems, recv_sems = refs[-5:]
+    streams = len(prefix_refs)
+    cols = prefix_refs[0].shape[1]
     width = streams * cols
     me = lax.axis_index("rows")
     barrier = pltpu.get_barrier_semaphore()
@@ -78,23 +80,8 @@
         return carry
 
     lax.fori_loop(0, count, greet, 0)
-    span = group * LANES
-
-    def masked(s, g):
-        columns = pl.ds(pl.multiple_of(g * span, span), span)
-        return jnp.where(keep_ref[s : s + 1, columns] != 0, events_ref[s, :, columns], 0.0)
-
-    totals = []
-    for s in range(streams):
-
-        def add(g, total, s=s):
-            values = masked(s, g)
-            parts = [values[:, i * LANES : (i + 1) * LANES] for i in range(group)]
-            while len(parts) > 1:
-                parts = [parts[i] + parts[i + 1] for i in range(0, len(parts), 2)]
-            return total + parts[0]
-
-        totals.append(lax.fori_loop(0, tiles // group, add, jnp.zeros((cols, LANES), F32), unroll=True))
+    last = iota((cols, LANES), 1) == LANES - 1
+    totals = [jnp.where(last, ref[tiles - 1], 0.0) for ref in prefix_refs]
     sums = lax.dot_general(
         jnp.ones((8, LANES), F32),
         jnp.concatenate(totals, axis=0),
@@ -132,25 +119,6 @@
 
     lax.fori_loop(0, count, send, 0)
 
-    shape = (2 * LANES, 2 * LANES)
-    weights = (((iota(shape, 0) & (LANES - 1)) <= iota(shape, 1)).astype(F32)).astype(BF16)
-    for s in range(1, streams):
-
-        def accumulate(g, total, s=s):
-            values = masked(s, g)
-            high = values.astype(BF16)
-            low = (values - high.astype(F32)).astype(BF16)
-            left = jnp.concatenate([high[:, i * LANES : (i + 1) * LANES] for i in range(group)], axis=0)
-            right = jnp.concatenate([low[:, i * LANES : (i + 1) * LANES] for i in range(group)], axis=0)
-            out = jnp.dot(jnp.concatenate([left, right], axis=1), weights, preferred_element_type=F32)
-            for i in range(group):
-                piece = out[i * cols : (i + 1) * cols]
-                prefix_ref[(s - 1) * tiles + g * group + i] = piece[:, :LANES] + total
-                total = total + piece[:, LANES:]
-            return total
-
-        lax.fori_loop(0, tiles // group, accumulate, jnp.zeros((cols, LANES), F32))
-
     def receive(j, carry):
         @pl.when(j < me)
         def _():
@@ -168,36 +136,6 @@
 
     lax.fori_loop(0, count, receive, 0)
     lax.fori_loop(0, count, finish, 0)
-
-
-def pack_kernel(s, tiles, scalars_ref, prefix_ref, slot_ref, *rest):
-    table_ref, send_ref = rest[-2:]
-    cols = prefix_ref.shape[1]
-    lane = iota((cols, LANES), 1)
-    current = jnp.zeros((cols, LANES), F32)
-    for t in range(tiles):
-        order = jnp.broadcast_to(slot_ref[s * tiles + t : s * tiles + t + 1, :], (cols, LANES))
-        packed = lane_gather(prefix_ref[(s - 1) * tiles + t], order)
-        begin = scalars_ref[0, s * tiles + t] + 1
-        block = begin // LANES
-        merged = jnp.where(lane >= begin - block * LANES, packed, current)
-        table_ref[block] = merged
-        if t == tiles - 1:
-            table_ref[block + 1] = packed
-        else:
-            following = (scalars_ref[0, s * tiles + t + 1] + 1) // LANES
-            current = jnp.where(following > block, packed, merged)
-    last = prefix_ref[s * tiles - 1]
-    total = lane_gather(last, jnp.full((cols, LANES), LANES - 1, I32))
-    base = scalars_ref[1, s * tiles] - SPAN
-    origin = base // LANES
-    offset = base - origin * LANES
-    turn = (lane + offset) & (LANES - 1)
-    below = table_ref[origin]
-    for m in range(SPAN // LANES):
-        above = table_ref[origin + m + 1]
-        send_ref[m] = lane_gather(jnp.where(lane >= offset, below, above), turn) - total
-        below = above
 
 
 def first_pack_kernel(s, tiles, group, scalars_ref, events_ref, keep_ref, slot_ref, *rest):
@@ -273,7 +211,7 @@
             block = begin // LANES
             mixed = jnp.where(lane >= begin - block * LANES, fetch(block), fetch(block + 1))
             order = jnp.broadcast_to(rank_ref[s * tiles + t : s * tiles + t + 1, :] & (LANES - 1), (cols, LANES))
-            running = prefix_ref[max(s - 1, 0) * tiles + t]
+            running = prefix_ref[t]
             mean = (running - lane_gather(mixed, order)) * (1.0 / SPAN)
             columns = slice(t * LANES, (t + 1) * LANES)
             means[:, columns] = mean
@@ -314,54 +252,40 @@
     )(keep)
 
     links = [(i, i + 1) for i in range(count - 1)]
-    first, table, send = pl.pallas_call(
-        functools.partial(first_pack_kernel, 0, tiles, group),
-        in_specs=[smem, vmem, vmem, vmem],
-        out_specs=[vmem] * 3,
-        out_shape=[
-            jax.ShapeDtypeStruct((tiles, cols, LANES), F32),
-            jax.ShapeDtypeStruct((tiles + 2, cols, LANES), F32),
-            jax.ShapeDtypeStruct((back, cols, LANES), F32),
-        ],
-        cost_estimate=cost,
-        compiler_params=params,
-        name="pack0",
-    )(scalars, events, keep, slot)
-    tables, tails = [table], [lax.ppermute(send, "rows", links)]
-
-    prefix, before = pl.pallas_call(
-        functools.partial(head_kernel, count, tiles, group),
-        in_specs=[smem, vmem, vmem, anywhere],
-        out_specs=[vmem, vmem],
-        out_shape=[
-            jax.ShapeDtypeStruct((everything - tiles, cols, LANES), F32),
-            jax.ShapeDtypeStruct((8, width), F32),
-        ],
+    prefixes, tables, tails = [], [], []
+    for s in range(streams):
+        prefix, table, send = pl.pallas_call(
+            functools.partial(first_pack_kernel, s, tiles, group),
+            in_specs=[smem, vmem, vmem, vmem] + [anywhere] * (s > 0),
+            out_specs=[vmem] * 3,
+            out_shape=[
+                jax.ShapeDtypeStruct((tiles, cols, LANES), F32),
+                jax.ShapeDtypeStruct((tiles + 2, cols, LANES), F32),
+                jax.ShapeDtypeStruct((back, cols, LANES), F32),
+            ],
+            cost_estimate=cost,
+            compiler_params=params,
+            name=f"pack{s}",
+        )(scalars, events, keep, slot, *tables[-1:])
+        prefixes.append(prefix)
+        tables.append(table)
+        tails.append(lax.ppermute(send, "rows", links))
+
+    before = pl.pallas_call(
+        functools.partial(head_kernel, count, tiles),
+        in_specs=[smem] + [vmem] * streams,
+        out_specs=vmem,
+        out_shape=jax.ShapeDtypeStruct((8, width), F32),
         scratch_shapes=[
             pltpu.VMEM((8, width), F32),
             pltpu.VMEM((count, 8, width), F32),
             pltpu.SemaphoreType.DMA((count,)),
             pltpu.SemaphoreType.DMA((count,)),
         ],
+        cost_estimate=cost,
         compiler_params=pltpu.CompilerParams(collective_id=0, has_side_effects=True, vmem_limit_bytes=GRANT),
         name="head",
-    )(scalars, events, keep, table)
-
-    for s in range(1, streams):
-        table, send = pl.pallas_call(
-            functools.partial(pack_kernel, s, tiles),
-            in_specs=[smem, vmem, vmem] + [anywhere] * (s > 0),
-            out_specs=[vmem, vmem],
-            out_shape=[
-                jax.ShapeDtypeStruct((tiles + 2, cols, LANES), F32),
-                jax.ShapeDtypeStruct((back, cols, LANES), F32),
-            ],
-            cost_estimate=cost,
-            compiler_params=params,
-            name=f"pack{s}",
-        )(scalars, prefix, slot, *tables[-1:])
-        tails.append(lax.ppermute(send, "rows", [(i, i + 1) for i in range(count - 1)]))
-        tables.append(table)
+    )(scalars, *prefixes)
 
     outs = ()
     for s in range(streams):
@@ -380,7 +304,7 @@
             cost_estimate=cost,
             compiler_params=params,
             name=f"spread{s}",
-        )(scalars, before, rank, prefix if s else first, tables[s], tails[s], *outs)
+        )(scalars, before, rank, prefixes[s], tables[s], tails[s], *outs)
     return tuple(outs)
 
 

time: 61.7 us -> 59.4 us (0.963)
  waiting for transfers between devices: 9.1 us -> 0.01 us
  Pallas kernels: 40.8 us -> 44 us
  starting transfers between devices: 7.79 us -> 10.8 us
    ppermute x4, waiting for transfers between devices: 9.1 us -> 0.01 us  [per_device(): tails.append(lax.ppermute(send, 'rows', links))]
    pallas_call x5, Pallas kernels: 29 us -> 32.3 us  [the longest x1 25.3 us: per_device(): pl.pallas_call(functools.partial(head_kernel, count, tiles), in_specs=[sm...]
    ppermute x4, starting transfers between devices: 7.79 us -> 10.8 us  [per_device(): tails.append(lax.ppermute(send, 'rows', links))]
    unnamed x6 -> x4, local copies, waits for them, and re-layouts: 3.09 us -> 3.08 us
  transfers between devices with their start and end apart: 4 -> 4, of which waited for: 3 -> 0; matrix products, arithmetic and copies ran while one was open for 0% -> 0% of each run, Pallas kernels for 57% -> 66%
where the time goes in v1:
time: 59.4 us; the launch traced here: 58.8 us
  Pallas kernels  44 us (74%)
  starting transfers between devices  10.8 us (18%)
  local copies, waits for them, and re-layouts  3.08 us (5%)
  between operations  0.77 us (1%)
    pallas_call x1, Pallas kernels, per_device(): pl.pallas_call(functools.partial(head_kernel, count, tiles), in_specs=[sm...  25.3 us
    ppermute x4, starting transfers between devices, per_device(): tails.append(lax.ppermute(send, 'rows', links))  10.8 us
    pallas_call x4, Pallas kernels, per_device(): pl.pallas_call(functools.partial(spread_kernel, s, tiles, group), in_spec...  10.8 us
    pallas_call x4, Pallas kernels, per_device(): pl.pallas_call(functools.partial(first_pack_kernel, s, tiles, group), in_...  7.01 us
    unnamed x4, local copies, waits for them, and re-layouts  3.08 us
  transfers between devices with their start and end apart: 4, of which 0 were waited for; matrix products, arithmetic and copies ran while one was open for 0% of the time, Pallas kernels for 66%

profile of v1, /device:TPU:32, one launch (start us, length us, event | category | flops | bytes accessed | tf_op | source)
XLA Modules:
  0.0 58.8 jit_solution(15507136680016052829)
XLA Ops:
  0.6 0.0 copy-start.1
  0.6 0.9 %copy-done.1 = s32[4,8192]{1,0:T(4,128)S(1)} copy-done((s32[4,8192]{1,0:T(4,128)S(1)}, s32[4,8192]{1,0:T(4,128)}, u32[]{:S(2)}) %copy-start.1) | copy-done | bytes 131096
  1.5 1.0 %index.1 = (s32[256,128]{1,0:T(8,128)S(1)}, s32[256,128]{1,0:T(8,128)S(1)}, s32[8,256]{1,0:T(8,128)S(1)}) custom-call(s32[4,8192]{1,0:T(4,128)S(1)} %copy-done.1), custom_call_target="tpu_custom_call" | custom-call | flops 1000000000 | bytes 8388608 | tf_op jit(solution)/shard_map/index/pallas_call | solution.py:241
  2.5 0.0 copy-start
  2.5 2.2 %copy-done = f32[4,32,8192]{2,1,0:T(8,128)S(1)} copy-done((f32[4,32,8192]{2,1,0:T(8,128)S(1)}, f32[4,32,8192]{2,1,0:T(8,128)}, u32[]{:S(2)}) %copy-start) | copy-done | bytes 4194328
  4.7 1.8 %pack0.1 = (f32[64,32,128]{2,1,0:T(8,128)S(1)}, f32[66,32,128]{2,1,0:T(8,128)S(1)}, f32[32,32,128]{2,1,0:T(8,128)S(1)}) custom-call(s32[8,256]{1,0:T(8,128)S(1)} %get-tuple-element.23.scalars_ref, f32[4,32,8192]{2,1,0:T(8,128)S(1)} %copy-done, s32[4,8192]{1,0:T(4,128)S(1)} %copy-done.1, s32[256,128]{1,0:T(8,128)S(1)} %get-tuple-element.24.slot_ref), custom_call_target="tpu_custom_call" | custom-call | flops 1000000000 | bytes 8388608 | tf_op jit(solution)/shard_map/pack0/pallas_call | solution.py:257
  6.5 1.9 %collective-permute-start.3 = (f32[32,32,128]{2,1,0:T(8,128)S(1)}, f32[32,32,128]{2,1,0:T(8,128)S(1)}, u32[]{:S(2)}, u32[]{:S(2)}) collective-permute-start(f32[32,32,128]{2,1,0:T(8,128)S(1)} %get-tuple-element.37), channel_id=1, source_target_pairs={{0,1},{1,2},{2,3},{3,4},{4,5},{5,6},{6,7},{7,8},{8,9},{9,10},{10,1... | collective-permute-start | bytes 1572872 | tf_op jit(solution)/shard_map/ppermute | solution.py:272
  8.4 1.8 %pack1.1 = (f32[64,32,128]{2,1,0:T(8,128)S(1)}, f32[66,32,128]{2,1,0:T(8,128)S(1)}, f32[32,32,128]{2,1,0:T(8,128)S(1)}) custom-call(s32[8,256]{1,0:T(8,128)S(1)} %get-tuple-element.23.scalars_ref, f32[4,32,8192]{2,1,0:T(8,128)S(1)} %copy-done, s32[4,8192]{1,0:T(4,128)S(1)} %copy-done.1, s32[256,128]{1,0:T(8,128)S(1)} %get-tuple-element.24.slot_ref, ...), custom_call_target="tpu_custom_call" | custom-call | flops 1000000000 | bytes 8388608 | tf_op jit(solution)/shard_map/pack1/pallas_call | solution.py:257
  10.1 3.5 %collective-permute-start.2 = (f32[32,32,128]{2,1,0:T(8,128)S(1)}, f32[32,32,128]{2,1,0:T(8,128)S(1)}, u32[]{:S(2)}, u32[]{:S(2)}) collective-permute-start(f32[32,32,128]{2,1,0:T(8,128)S(1)} %get-tuple-element.36), channel_id=1, source_target_pairs={{0,1},{1,2},{2,3},{3,4},{4,5},{5,6},{6,7},{7,8},{8,9},{9,10},{10,1... | collective-permute-start | bytes 1572872 | tf_op jit(solution)/shard_map/ppermute | solution.py:272
  13.7 1.8 %pack2.1 = (f32[64,32,128]{2,1,0:T(8,128)S(1)}, f32[66,32,128]{2,1,0:T(8,128)S(1)}, f32[32,32,128]{2,1,0:T(8,128)S(1)}) custom-call(s32[8,256]{1,0:T(8,128)S(1)} %get-tuple-element.23.scalars_ref, f32[4,32,8192]{2,1,0:T(8,128)S(1)} %copy-done, s32[4,8192]{1,0:T(4,128)S(1)} %copy-done.1, s32[256,128]{1,0:T(8,128)S(1)} %get-tuple-element.24.slot_ref, ...), custom_call_target="tpu_custom_call" | custom-call | flops 1000000000 | bytes 8388608 | tf_op jit(solution)/shard_map/pack2/pallas_call | solution.py:257
  15.4 1.9 %collective-permute-start.1 = (f32[32,32,128]{2,1,0:T(8,128)S(1)}, f32[32,32,128]{2,1,0:T(8,128)S(1)}, u32[]{:S(2)}, u32[]{:S(2)}) collective-permute-start(f32[32,32,128]{2,1,0:T(8,128)S(1)} %get-tuple-element.35), channel_id=1, source_target_pairs={{0,1},{1,2},{2,3},{3,4},{4,5},{5,6},{6,7},{7,8},{8,9},{9,10},{10,1... | collective-permute-start | bytes 1572872 | tf_op jit(solution)/shard_map/ppermute | solution.py:272
  17.3 1.8 %pack3.1 = (f32[64,32,128]{2,1,0:T(8,128)S(1)}, f32[66,32,128]{2,1,0:T(8,128)S(1)}, f32[32,32,128]{2,1,0:T(8,128)S(1)}) custom-call(s32[8,256]{1,0:T(8,128)S(1)} %get-tuple-element.23.scalars_ref, f32[4,32,8192]{2,1,0:T(8,128)S(1)} %copy-done, s32[4,8192]{1,0:T(4,128)S(1)} %copy-done.1, s32[256,128]{1,0:T(8,128)S(1)} %get-tuple-element.24.slot_ref, ...), custom_call_target="tpu_custom_call" | custom-call | flops 1000000000 | bytes 8388608 | tf_op jit(solution)/shard_map/pack3/pallas_call | solution.py:257
  19.1 3.5 %collective-permute-start = (f32[32,32,128]{2,1,0:T(8,128)S(1)}, f32[32,32,128]{2,1,0:T(8,128)S(1)}, u32[]{:S(2)}, u32[]{:S(2)}) collective-permute-start(f32[32,32,128]{2,1,0:T(8,128)S(1)} %get-tuple-element.34), channel_id=1, source_target_pairs={{0,1},{1,2},{2,3},{3,4},{4,5},{5,6},{6,7},{7,8},{8,9},{9,10},{10,1... | collective-permute-start | bytes 1572872 | tf_op jit(solution)/shard_map/ppermute | solution.py:272
  22.6 25.3 %head.1.before_ref = f32[8,128]{1,0:T(8,128)S(1)} custom-call(s32[8,256]{1,0:T(8,128)S(1)} %get-tuple-element.23.scalars_ref, f32[64,32,128]{2,1,0:T(8,128)S(1)} %get-tuple-element.25.refs_0_.prefix_ref, f32[64,32,128]{2,1,0:T(8,128)S(1)} %get-tuple-element.27.refs_1_.prefix_ref, f32[64,32,128]{2,1,0:T(8,128)S(1)} %get-tuple-element.29.refs_2_.prefix_ref, ...), custom_call_target="tpu_custom_call" | custom-call | flops 1000000000 | bytes 8388608 | tf_op jit(solution)/shard_map/head/pallas_call | solution.py:274
  47.9 0.0 collective-permute-done.3.tail_ref
  47.9 2.7 %spread0.1 = (f32[4,32,8192]{2,1,0:T(8,128)}, f32[4,32,8192]{2,1,0:T(8,128)}) custom-call(s32[8,256]{1,0:T(8,128)S(1)} %get-tuple-element.23.scalars_ref, f32[8,128]{1,0:T(8,128)S(1)} %head.1.before_ref, s32[256,128]{1,0:T(8,128)S(1)} %get-tuple-element.32.rank_ref, f32[64,32,128]{2,1,0:T(8,128)S(1)} %get-tuple-element.25.refs_0_.prefix_ref, ...), custom_call_target="tpu_custom_call" | custom-call | flops 1000000000 | bytes 8388608 | tf_op jit(solution)/shard_map/spread0/pallas_call | solution.py:292
  50.6 0.0 collective-permute-done.2.tail_ref
  50.7 2.7 %spread1.1 = (f32[4,32,8192]{2,1,0:T(8,128)}, f32[4,32,8192]{2,1,0:T(8,128)}) custom-call(s32[8,256]{1,0:T(8,128)S(1)} %get-tuple-element.23.scalars_ref, f32[8,128]{1,0:T(8,128)S(1)} %head.1.before_ref, s32[256,128]{1,0:T(8,128)S(1)} %get-tuple-element.32.rank_ref, ...), custom_call_target="tpu_custom_call", output_to_operand_aliasing={{0}: (6, {}), {1}: (7, {})} | custom-call | flops 1000000000 | bytes 8388608 | tf_op jit(solution)/shard_map/spread1/pallas_call | solution.py:292
  53.3 0.0 collective-permute-done.1.tail_ref
  53.4 2.7 %spread2.1 = (f32[4,32,8192]{2,1,0:T(8,128)}, f32[4,32,8192]{2,1,0:T(8,128)}) custom-call(s32[8,256]{1,0:T(8,128)S(1)} %get-tuple-element.23.scalars_ref, f32[8,128]{1,0:T(8,128)S(1)} %head.1.before_ref, s32[256,128]{1,0:T(8,128)S(1)} %get-tuple-element.32.rank_ref, ...), custom_call_target="tpu_custom_call", output_to_operand_aliasing={{0}: (6, {}), {1}: (7, {})} | custom-call | flops 1000000000 | bytes 8388608 | tf_op jit(solution)/shard_map/spread2/pallas_call | solution.py:292
  56.1 0.0 collective-permute-done.tail_ref
  56.1 2.7 %spread3.1 = (f32[4,32,8192]{2,1,0:T(8,128)}, f32[4,32,8192]{2,1,0:T(8,128)}) custom-call(s32[8,256]{1,0:T(8,128)S(1)} %get-tuple-element.23.scalars_ref, f32[8,128]{1,0:T(8,128)S(1)} %head.1.before_ref, s32[256,128]{1,0:T(8,128)S(1)} %get-tuple-element.32.rank_ref, ...), custom_call_target="tpu_custom_call", output_to_operand_aliasing={{0}: (6, {}), {1}: (7, {})} | custom-call | flops 1000000000 | bytes 8388608 | tf_op jit(solution)/shard_map/spread3/pallas_call | solution.py:292
Async XLA Ops:
  0.6 0.9 %copy-start.1 = (s32[4,8192]{1,0:T(4,128)S(1)}, s32[4,8192]{1,0:T(4,128)}, u32[]{:S(2)}) copy-start(s32[4,8192]{1,0:T(4,128)} %keep_ref.9) | copy-start | bytes 393220
  2.5 2.2 %copy-start = (f32[4,32,8192]{2,1,0:T(8,128)S(1)}, f32[4,32,8192]{2,1,0:T(8,128)}, u32[]{:S(2)}) copy-start(f32[4,32,8192]{2,1,0:T(8,128)} %events_ref.7) | copy-start | bytes 12582916
  6.5 41.5 %collective-permute-start.3 = (f32[32,32,128]{2,1,0:T(8,128)S(1)}, f32[32,32,128]{2,1,0:T(8,128)S(1)}, u32[]{:S(2)}, u32[]{:S(2)}) collective-permute-start(f32[32,32,128]{2,1,0:T(8,128)S(1)} %get-tuple-element.37), channel_id=1, source_target_pairs={{0,1},{1,2},{2,3},{3,4},{4,5},{5,6},{6,7},{7,8},{8,9},{9,10},{10,1... | collective-permute-start | bytes 1572872 | tf_op jit(solution)/shard_map/ppermute | solution.py:272
  10.1 40.5 %collective-permute-start.2 = (f32[32,32,128]{2,1,0:T(8,128)S(1)}, f32[32,32,128]{2,1,0:T(8,128)S(1)}, u32[]{:S(2)}, u32[]{:S(2)}) collective-permute-start(f32[32,32,128]{2,1,0:T(8,128)S(1)} %get-tuple-element.36), channel_id=1, source_target_pairs={{0,1},{1,2},{2,3},{3,4},{4,5},{5,6},{6,7},{7,8},{8,9},{9,10},{10,1... | collective-permute-start | bytes 1572872 | tf_op jit(solution)/shard_map/ppermute | solution.py:272
  15.4 37.9 %collective-permute-start.1 = (f32[32,32,128]{2,1,0:T(8,128)S(1)}, f32[32,32,128]{2,1,0:T(8,128)S(1)}, u32[]{:S(2)}, u32[]{:S(2)}) collective-permute-start(f32[32,32,128]{2,1,0:T(8,128)S(1)} %get-tuple-element.35), channel_id=1, source_target_pairs={{0,1},{1,2},{2,3},{3,4},{4,5},{5,6},{6,7},{7,8},{8,9},{9,10},{10,1... | collective-permute-start | bytes 1572872 | tf_op jit(solution)/shard_map/ppermute | solution.py:272
  19.1 37.0 %collective-permute-start = (f32[32,32,128]{2,1,0:T(8,128)S(1)}, f32[32,32,128]{2,1,0:T(8,128)S(1)}, u32[]{:S(2)}, u32[]{:S(2)}) collective-permute-start(f32[32,32,128]{2,1,0:T(8,128)S(1)} %get-tuple-element.34), channel_id=1, source_target_pairs={{0,1},{1,2},{2,3},{3,4},{4,5},{5,6},{6,7},{7,8},{8,9},{9,10},{10,1... | collective-permute-start | bytes 1572872 | tf_op jit(solution)/shard_map/ppermute | solution.py:272
